TPU v7x, 128 devices: a whole 4x4x4 slice. The times are simulated.
128 devices in a mesh: seq: 8 (over z_hi, x), batch: 16 (over z_lo, y, core).
Axes of the slice: x: 4, y: 4, z: 4 (z_hi: 2, z_lo: 2; z = z_hi * 2 + z_lo), core: 2. Of those that a mesh axis runs over, the one named last changes fastest.
Arguments:
- attn_out: bfloat16 [65536, 2560], P(('seq', 'batch')), may hold values from -200 to 200
- out_grad: bfloat16 [65536, 2560], P(('seq', 'batch')), may hold values from -6 to 6
- master: float32 [2560, 2560], P(('seq', 'batch')), may hold values from -0.125 to 0.125
- moment_one: float32 [2560, 2560], P(('seq', 'batch')), may hold values from -4 to 4
- moment_two: float32 [2560, 2560], P(('seq', 'batch')), may hold values from 0.002 to 0.05
Outputs:
- input_grad: bfloat16 [65536, 2560], P(('seq', 'batch'))
- new_master: float32 [2560, 2560], P(('seq', 'batch'))
- new_moment_one: float32 [2560, 2560], P(('seq', 'batch'))
- new_moment_two: float32 [2560, 2560], P(('seq', 'batch'))
All inputs are finite; a program needn't handle non-finite values.
Results may differ from a plain program's by a relative error of at most 0.01.
Values may be sent and summed in bfloat16 or wider, within the bound.
A program may use at most 128 MiB of HBM per device.

v0:
```python
import jax
import jax.numpy as jnp
from jax import lax
from jax.sharding import Mesh
from jax.sharding import PartitionSpec as P

DIN = 2560
DOUT = 2560
GRAD_BLOCKS = 4
STEP = 10
BATCH = ("batch_0", "batch_1", "batch_2")
SEQ = ("seq_0", "seq_1")
SEQ_BATCH = ("seq_0", "seq_1", "batch_0", "batch_1", "batch_2")


def laid_out(pieces, dim):
    pieces = jnp.moveaxis(pieces, 0, dim)
    lengths = pieces.shape
    return pieces.reshape(*lengths[:dim], lengths[dim] * lengths[dim + 1], *lengths[dim + 2 :])


def copy_for_each(value, axis):
    devices = lax.axis_size(axis)
    return lax.all_to_all(
        jnp.broadcast_to(value[None], (devices, *value.shape)), axis, 0, 0, tiled=True
    )


def gather_directly(value, axis, dim):
    return laid_out(copy_for_each(value, axis), dim)


def by_axis(value, axes):
    for axis in axes:
        value = lax.psum(value, axis)
    return value


def on_device(attn_out, out_grad, master, moment_one, moment_two):
    shard_weight = master.astype(jnp.bfloat16)
    grouped = gather_directly(shard_weight, BATCH, 0)
    projected = lax.dot_general(
        out_grad,
        lax.all_gather(grouped, SEQ, axis=0, tiled=True),
        (((1,), (1,)), ((), ())),
        preferred_element_type=jnp.float32,
    )
    input_grad = projected.astype(jnp.bfloat16)
    block_width = out_grad.shape[1] // GRAD_BLOCKS
    grad_parts = []
    for block in range(GRAD_BLOCKS):
        grad_cols = out_grad[:, block * block_width : (block + 1) * block_width]
        grad_parts.append(
            lax.psum_scatter(
                lax.dot_general(
                    attn_out,
                    grad_cols,
                    (((0,), (0,)), ((), ())),
                    preferred_element_type=jnp.float32,
                ).astype(jnp.bfloat16),
                SEQ_BATCH,
                scatter_dimension=0,
                tiled=True,
            ).astype(jnp.float32)
        )
    weight_grad = jnp.concatenate(grad_parts, axis=1)
    squares = by_axis(jnp.sum(weight_grad * weight_grad), SEQ_BATCH)
    grad_norm = jnp.sqrt(squares) + 1e-06
    limit = jnp.sqrt(jnp.float32(DIN * DOUT))
    clipped = weight_grad * jnp.minimum(jnp.float32(1.0), limit / grad_norm)
    new_one = 0.9 * moment_one + 0.1 * clipped
    new_two = 0.999 * moment_two + 0.001 * clipped * clipped
    first_hat = new_one / (1.0 - 0.9**STEP)
    second_hat = new_two / (1.0 - 0.999**STEP)
    new_master = master - 0.01 * (first_hat / (jnp.sqrt(second_hat) + 1e-08) + 0.1 * master)
    return (input_grad, new_master, new_one, new_two)


def solution(mesh):
    finer = Mesh(
        mesh.devices.reshape(2, 4, 2, 4, 2), ("seq_0", "seq_1", "batch_0", "batch_1", "batch_2")
    )
    in_specs = (
        P(SEQ_BATCH, None),
        P(SEQ_BATCH, None),
        P(SEQ_BATCH, None),
        P(SEQ_BATCH, None),
        P(SEQ_BATCH, None),
    )
    out_specs = (P(SEQ_BATCH, None), P(SEQ_BATCH, None), P(SEQ_BATCH, None), P(SEQ_BATCH, None))
    return jax.shard_map(
        on_device, mesh=finer, in_specs=in_specs, out_specs=out_specs, check_vma=False
    )
```

profile of v0, /device:TPU:0, one launch (start us, length us, event | category | flops | bytes accessed | tf_op | source)
XLA Modules:
  0.0 438.9 jit_solution(13695303821592365688)
XLA Ops:
  7.2 0.0 all-reduce.7.cloned.1.call-start
  7.2 1.7 copy-done
  8.9 5.1 %convolution_convert_fusion = bf16[2560,640]{1,0:T(8,128)(2,1)} fusion(bf16[512,2560]{1,0:T(8,128)(2,1)S(1)} %copy-done, bf16[512,2560]{1,0:T(8,128)(2,1)} %param.6), kind=kOutput, calls=%fused_computation | convolution fusion | flops 1679360000 | bytes 6553600 | tf_op jit(solution)/shard_map/dot_general | solution.py:55
  14.1 4.0 convolution_convert_fusion.1
  18.0 4.0 convolution_convert_fusion.2
  22.0 4.0 convolution_convert_fusion.3
  26.0 0.0 all-reduce.7.cloned.1.call-update
  26.0 0.0 all-gather.2.cloned.1.call-start
  26.1 173.5 %all-reduce.7.cloned.1.call-done = (bf16[2560,640]{1,0:T(8,128)(2,1)}, bf16[2560,640]{1,0:T(8,128)(2,1)}, bf16[2560,640]{1,0:T(8,128)(2,1)}, bf16[2560,640]{1,0:T(8,128)(2,1)}) async-done(((bf16[2560,640]{1,0:T(8,128)(2,1)}, bf16[2560,640]{1,0:T(8,128)(2,1)}, bf16[2560,640]{1,0:T(8,128)(2,1)}, bf16[2560,640]{1,0:T(8,128)(2,1)}), (bf16[2560,640]{1,0:T(8,128)(2,1)}, bf16[2560,640]{1,0:T(8,128)(2,1)}, ...) | async-done | bytes 13107216
  199.6 0.8 constant_dynamic-slice_fusion.2
  200.5 0.8 constant_dynamic-slice_fusion
  201.3 0.7 fusion.6
  202.0 7.0 %psum.35 = f32[]{:T(128)} all-reduce(f32[]{:T(128)} %fusion.6), channel_id=1, replica_groups=mesh['seq_0'=2,'seq_1'=4,'batch_0'=2,'batch_1'=4,'batch_2'=2] {'seq_0'}, use_global_device_ids=true, to_apply=%region_5.0 | all-reduce | flops 1 | bytes 8 | tf_op jit(solution)/shard_map/psum | solution.py:35
  209.0 10.4 %psum.36 = f32[]{:T(128)} all-reduce(f32[]{:T(128)} %psum.35), channel_id=1, replica_groups=mesh['seq_0'=2,'seq_1'=4,'batch_0'=2,'batch_1'=4,'batch_2'=2] {'seq_1'}, use_global_device_ids=true, to_apply=%region_6.0 | all-reduce | flops 1 | bytes 8 | tf_op jit(solution)/shard_map/psum | solution.py:35
  219.5 5.5 %psum.37 = f32[]{:T(128)} all-reduce(f32[]{:T(128)} %psum.36), channel_id=1, replica_groups=mesh['seq_0'=2,'seq_1'=4,'batch_0'=2,'batch_1'=4,'batch_2'=2] {'batch_0'}, use_global_device_ids=true, to_apply=%region_7.0 | all-reduce | flops 1 | bytes 8 | tf_op jit(solution)/shard_map/psum | solution.py:35
  225.0 10.7 %psum.38 = f32[]{:T(128)} all-reduce(f32[]{:T(128)} %psum.37), channel_id=1, replica_groups=mesh['seq_0'=2,'seq_1'=4,'batch_0'=2,'batch_1'=4,'batch_2'=2] {'batch_1'}, use_global_device_ids=true, to_apply=%region_8.0 | all-reduce | flops 1 | bytes 8 | tf_op jit(solution)/shard_map/psum | solution.py:35
  235.7 3.1 psum.39
  239.6 1.0 multiply_subtract_fusion
  240.5 0.1 broadcast_in_dim.2
  240.7 29.3 %all_to_all.5 = bf16[16,20,2560]{2,1,0:T(8,128)(2,1)} all-to-all(bf16[16,20,2560]{2,1,0:T(8,128)(2,1)S(1)} %broadcast_in_dim.2), channel_id=1, replica_groups=mesh['seq_0'=2,'seq_1'=4,'batch_0'=2,'batch_1'=4,'batch_2'=2] {'batch_0'..., dimensions={0} | all-to-all | bytes 3276800 | tf_op jit(solution)/shard_map/all_to_all | solution.py:24
  270.0 3.5 reshape.12
  273.5 0.0 all-gather.2.cloned.1.call-update
  273.5 146.7 %all-gather.2.cloned.1.call-done = bf16[2560,2560]{1,0:T(8,128)(2,1)} async-done(((bf16[320,2560]{1,0:T(8,128)(2,1)}), bf16[2560,2560]{1,0:T(8,128)(2,1)}) %all-gather.2.cloned.1.call-update) | async-done | bytes 13107216 | tf_op jit(solution)/shard_map/all_gather | solution.py:44
  420.2 11.9 %convolution_convert_fusion.4 = bf16[512,2560]{1,0:T(8,128)(2,1)} fusion(bf16[512,2560]{1,0:T(8,128)(2,1)} %param.6, bf16[2560,2560]{1,0:T(8,128)(2,1)} %all-gather.2.cloned.1.call-done), kind=kOutput, calls=%fused_computation.4 | convolution fusion | flops 6712197120 | bytes 18350080 | tf_op jit(solution)/shard_map/dot_general | solution.py:42
  (9 shorter events, 0.0 us)
Async XLA Ops:
  7.2 1.7 copy-start
  7.2 192.5 %all-reduce.7.cloned.1.call-start = ((), (), s32[]{:S(2)}) async-start(), calls=%async_computation.2 | async-start | bytes 26214400
  8.9 5.2 %copy-start.4 = (bf16[512,2560]{1,0:T(8,128)(2,1)S(1)}, bf16[512,2560]{1,0:T(8,128)(2,1)}, u32[]{:S(2)}) copy-start(bf16[512,2560]{1,0:T(8,128)(2,1)} %param.6) | copy-start | bytes 7864324
  26.0 213.5 %copy-start.1 = (f32[20,2560]{1,0:T(8,128)S(1)}, f32[20,2560]{1,0:T(8,128)}, u32[]{:S(2)}) copy-start(f32[20,2560]{1,0:T(8,128)} %param.7) | copy-start | bytes 614404
  26.0 213.5 %copy-start.2 = (f32[20,2560]{1,0:T(8,128)S(1)}, f32[20,2560]{1,0:T(8,128)}, u32[]{:S(2)}) copy-start(f32[20,2560]{1,0:T(8,128)} %param.8) | copy-start | bytes 614404
  26.0 213.5 %copy-start.3 = (f32[20,2560]{1,0:T(8,128)S(1)}, f32[20,2560]{1,0:T(8,128)}, u32[]{:S(2)}) copy-start(f32[20,2560]{1,0:T(8,128)} %param.9) | copy-start | bytes 614404
  26.0 394.1 %all-gather.2.cloned.1.call-start = ((), (), s32[]{:S(2)}) async-start(), calls=%async_computation.1 | async-start | bytes 14745600 | tf_op jit(solution)/shard_map/all_gather | solution.py:44
Sparse Core Ops, SparseCore 0:
  26.2 173.4 all-reduce.6
  273.7 146.4 all-gather.1
where the time goes:
time: 439 us
  waiting for transfers between devices  320 us (73%)
  blocking collectives  66.2 us (15%)
  matrix products  29 us (7%)
  between operations  14.8 us (3%)
  local copies, waits for them, and re-layouts  6.99 us (2%)
    unnamed x3, waiting for transfers between devices  174 us
    all_gather x1, waiting for transfers between devices, on_device(): lax.all_gather(grouped, SEQ, axis=0, tiled=True)  147 us
    psum x5, blocking collectives, by_axis(): value = lax.psum(value, axis)  36.8 us
    all_to_all x1, blocking collectives, copy_for_each(): lax.all_to_all(jnp.broadcast_to(value[None], (devices, *value.shape)), ax...  29.3 us
    dot_general x4, matrix products, on_device(): lax.dot_general(attn_out, grad_cols, (((0,), (0,)), ((), ())), preferred_...  17.1 us
    dot_general x1, matrix products, on_device(): lax.dot_general(out_grad, lax.all_gather(grouped, SEQ, axis=0, tiled=True...  11.9 us
  transfers between devices with their start and end apart: 2, of which 2 were waited for; matrix products, arithmetic and copies ran while one was open for 0% of the time, Pallas kernels for 0%

commit v1 on v0

--- a/solution.py
+++ b/solution.py
@@ -32,7 +32,7 @@
 
 def by_axis(value, axes):
     for axis in axes:
-        value = lax.psum(value, axis)
+        value = jnp.sum(lax.all_gather(value, axis), axis=0)
     return value
 
 

time: 439 us -> 449 us (1.023)
  local copies, waits for them, and re-layouts: 6.99 us -> 17.5 us
    psum x5 -> x0, blocking collectives: 36.8 us -> none  [by_axis(): value = lax.psum(value, axis)]
    unnamed x0 -> x5, blocking collectives: none -> 33.7 us
    unnamed x12 -> x37, local copies, waits for them, and re-layouts: 3.35 us -> 13.8 us
where the time goes in v1:
time: 449 us; the launch traced here: 448 us
  waiting for transfers between devices  319 us (71%)
  blocking collectives  63 us (14%)
  matrix products  29 us (6%)
  local copies, waits for them, and re-layouts  17.5 us (4%)
  between operations  14.9 us (3%)
  other arithmetic  4.67 us (1%)
    unnamed x3, waiting for transfers between devices  172 us
    all_gather x1, waiting for transfers between devices, on_device(): lax.all_gather(grouped, SEQ, axis=0, tiled=True)  147 us
    unnamed x5, blocking collectives  33.7 us
    all_to_all x1, blocking collectives, copy_for_each(): lax.all_to_all(jnp.broadcast_to(value[None], (devices, *value.shape)), ax...  29.3 us
    dot_general x4, matrix products, on_device(): lax.dot_general(attn_out, grad_cols, (((0,), (0,)), ((), ())), preferred_...  17.1 us
    unnamed x37, local copies, waits for them, and re-layouts  13.8 us
    dot_general x1, matrix products, on_device(): lax.dot_general(out_grad, lax.all_gather(grouped, SEQ, axis=0, tiled=True...  11.9 us
  transfers between devices with their start and end apart: 2, of which 2 were waited for; matrix products, arithmetic and copies ran while one was open for 0% of the time, Pallas kernels for 0%

profile of v1, /device:TPU:0, one launch (start us, length us, event | category | flops | bytes accessed | tf_op | source)
XLA Modules:
  0.0 448.2 jit_solution(2176065000952740465)
XLA Ops:
  7.2 1.7 copy-done
  8.9 5.1 %convolution_convert_fusion = bf16[2560,640]{1,0:T(8,128)(2,1)} fusion(bf16[512,2560]{1,0:T(8,128)(2,1)S(1)} %copy-done, bf16[512,2560]{1,0:T(8,128)(2,1)} %param.6), kind=kOutput, calls=%fused_computation | convolution fusion | flops 1679360000 | bytes 6553600 | tf_op jit(solution)/shard_map/dot_general | solution.py:55
  14.1 4.0 convolution_convert_fusion.1
  18.0 4.0 convolution_convert_fusion.2
  22.0 4.0 convolution_convert_fusion.3
  27.3 172.4 %all-reduce.12.cloned.1.call-done = (bf16[2560,640]{1,0:T(8,128)(2,1)}, bf16[2560,640]{1,0:T(8,128)(2,1)}, bf16[2560,640]{1,0:T(8,128)(2,1)}, bf16[2560,640]{1,0:T(8,128)(2,1)}) async-done(((bf16[2560,640]{1,0:T(8,128)(2,1)}, bf16[2560,640]{1,0:T(8,128)(2,1)}, bf16[2560,640]{1,0:T(8,128)(2,1)}, bf16[2560,640]{1,0:T(8,128)(2,1)}), (bf16[2560,640]{1,0:T(8,128)(2,1)}, bf16[2560,640]{1,0:T(8,128)(2,1)}, ...) | async-done | bytes 13107216
  199.7 0.8 constant_dynamic-slice_fusion.2
  200.5 0.8 constant_dynamic-slice_fusion
  201.4 0.7 fusion.6
  202.0 1.4 dynamic-update-slice
  204.0 6.4 %all-reduce = f32[2]{0:T(128)S(1)} all-reduce(f32[2]{0:T(128)S(1)} %dynamic-update-slice), channel_id=1, replica_groups=mesh['seq_0'=2,'seq_1'=4,'batch_0'=2,'batch_1'=4,'batch_2'=2] {'seq_0'}, use_global_device_ids=true, to_apply=%add | all-reduce | flops 2 | bytes 16
  211.0 1.4 dynamic-update-slice.1
  213.0 9.8 %all-reduce.1 = f32[4]{0:T(128)S(1)} all-reduce(f32[4]{0:T(128)S(1)} %dynamic-update-slice.1), channel_id=1, replica_groups=mesh['seq_0'=2,'seq_1'=4,'batch_0'=2,'batch_1'=4,'batch_2'=2] {'seq_1'}, use_global_device_ids=true, to_apply=%add.1 | all-reduce | flops 4 | bytes 32
  223.4 1.4 dynamic-update-slice.2
  225.4 4.9 %all-reduce.2 = f32[2]{0:T(128)S(1)} all-reduce(f32[2]{0:T(128)S(1)} %dynamic-update-slice.2), channel_id=1, replica_groups=mesh['seq_0'=2,'seq_1'=4,'batch_0'=2,'batch_1'=4,'batch_2'=2] {'batch_0'}, use_global_device_ids=true, to_apply=%add.2 | all-reduce | flops 2 | bytes 16
  230.9 1.4 dynamic-update-slice.3
  232.9 10.1 %all-reduce.3 = f32[4]{0:T(128)S(1)} all-reduce(f32[4]{0:T(128)S(1)} %dynamic-update-slice.3), channel_id=1, replica_groups=mesh['seq_0'=2,'seq_1'=4,'batch_0'=2,'batch_1'=4,'batch_2'=2] {'batch_1'}, use_global_device_ids=true, to_apply=%add.3 | all-reduce | flops 4 | bytes 32
  243.6 1.4 dynamic-update-slice.4
  245.0 2.4 all-reduce.4
  248.8 1.0 multiply_subtract_fusion
  249.9 29.3 %all_to_all.5 = bf16[16,20,2560]{2,1,0:T(8,128)(2,1)} all-to-all(bf16[16,20,2560]{2,1,0:T(8,128)(2,1)S(1)} %broadcast_in_dim.2), channel_id=1, replica_groups=mesh['seq_0'=2,'seq_1'=4,'batch_0'=2,'batch_1'=4,'batch_2'=2] {'batch_0'..., dimensions={0} | all-to-all | bytes 3276800 | tf_op jit(solution)/shard_map/all_to_all | solution.py:24
  279.3 3.5 reshape.12
  282.8 146.7 %all-gather.2.cloned.1.call-done = bf16[2560,2560]{1,0:T(8,128)(2,1)} async-done(((bf16[320,2560]{1,0:T(8,128)(2,1)}), bf16[2560,2560]{1,0:T(8,128)(2,1)}) %all-gather.2.cloned.1.call-update) | async-done | bytes 13107216 | tf_op jit(solution)/shard_map/all_gather | solution.py:44
  429.5 11.9 %convolution_convert_fusion.4 = bf16[512,2560]{1,0:T(8,128)(2,1)} fusion(bf16[512,2560]{1,0:T(8,128)(2,1)} %param.6, bf16[2560,2560]{1,0:T(8,128)(2,1)} %all-gather.2.cloned.1.call-done), kind=kOutput, calls=%fused_computation.4 | convolution fusion | flops 6712197120 | bytes 18350080 | tf_op jit(solution)/shard_map/dot_general | solution.py:42
  (39 shorter events, 6.7 us)
Async XLA Ops:
  7.2 1.7 copy-start
  7.2 192.5 %all-reduce.12.cloned.1.call-start = ((), (), s32[]{:S(2)}) async-start(), calls=%async_computation.2 | async-start | bytes 26214400
  8.9 5.2 %copy-start.4 = (bf16[512,2560]{1,0:T(8,128)(2,1)S(1)}, bf16[512,2560]{1,0:T(8,128)(2,1)}, u32[]{:S(2)}) copy-start(bf16[512,2560]{1,0:T(8,128)(2,1)} %param.6) | copy-start | bytes 7864324
  26.0 0.7 copy-start.9
  26.0 177.4 %copy-start.8 = (u32[128]{0:T(128)S(1)}, u32[128]{0:T(128)}, u32[]{:S(2)}) copy-start(u32[128]{0:T(128)} %constant.36) | copy-start | bytes 1540
  26.0 186.4 %copy-start.7 = (u32[128]{0:T(128)S(1)}, u32[128]{0:T(128)}, u32[]{:S(2)}) copy-start(u32[128]{0:T(128)} %constant.41) | copy-start | bytes 1540
  26.0 198.8 %copy-start.6 = (u32[128]{0:T(128)S(1)}, u32[128]{0:T(128)}, u32[]{:S(2)}) copy-start(u32[128]{0:T(128)} %constant.46) | copy-start | bytes 1540
  26.0 206.3 %copy-start.5 = (u32[128]{0:T(128)S(1)}, u32[128]{0:T(128)}, u32[]{:S(2)}) copy-start(u32[128]{0:T(128)} %constant.51) | copy-start | bytes 1540
  26.0 222.8 %copy-start.1 = (f32[20,2560]{1,0:T(8,128)S(1)}, f32[20,2560]{1,0:T(8,128)}, u32[]{:S(2)}) copy-start(f32[20,2560]{1,0:T(8,128)} %param.7) | copy-start | bytes 614404
  26.1 222.8 %copy-start.2 = (f32[20,2560]{1,0:T(8,128)S(1)}, f32[20,2560]{1,0:T(8,128)}, u32[]{:S(2)}) copy-start(f32[20,2560]{1,0:T(8,128)} %param.8) | copy-start | bytes 614404
  26.1 222.7 %copy-start.3 = (f32[20,2560]{1,0:T(8,128)S(1)}, f32[20,2560]{1,0:T(8,128)}, u32[]{:S(2)}) copy-start(f32[20,2560]{1,0:T(8,128)} %param.9) | copy-start | bytes 614404
  26.1 403.4 %all-gather.2.cloned.1.call-start = ((), (), s32[]{:S(2)}) async-start(), calls=%async_computation.1 | async-start | bytes 14745600 | tf_op jit(solution)/shard_map/all_gather | solution.py:44
Sparse Core Ops, SparseCore 0:
  26.2 173.4 all-reduce.11
  282.9 146.4 all-gather.1
